TPU v7x, 128 devices: a whole 4x4x4 slice. The times are simulated.
128 devices in a mesh: dp: 32 (over x, z, core), tensor: 4 (over y).
Axes of the slice: x: 4, y: 4, z: 4, core: 2. Of those that a mesh axis runs over, the one named last changes fastest.
Arguments:
- tokens: bfloat16 [2, 2048, 4096], P(None, 'dp', 'tensor'), may hold values from -6 to 6
- routes: int32 [2, 2048, 2], P(None, 'dp'), may hold values from 0 to 7, all different within a row; in each aligned block of 64 rows (0 to 63, 64 to 127, ..., all dimensions but the last counted through in order) at most 20 rows name the same one
- probs: float32 [2, 2048, 8], P(None, 'dp'), may hold values from 0 to 1, as said below
- w_gate: bfloat16 [32, 4096, 3584], P('dp', None, 'tensor'), may hold values from -0.09375 to 0.09375
- w_up: bfloat16 [32, 4096, 3584], P('dp', None, 'tensor'), may hold values from -0.09375 to 0.09375
- w_down: bfloat16 [32, 3584, 4096], P('dp', 'tensor'), may hold values from -0.046875 to 0.046875
Outputs:
- mixed: bfloat16 [2, 2048, 4096], P(None, 'dp', 'tensor')
- aux_loss: float32 [2, 8], replicated
Inputs may be any that keep to these rules, and one draw needn't show every extreme that they name: `routes`: in each aligned block of 64 rows (the rows of one index of dp in one micro-batch) no expert is named in more than 20 entries; the 2 experts of a row differ. `probs`: each row is positive and sums to one.
All inputs are finite; a program needn't handle non-finite values.
Results may differ from a plain program's by a relative error of at most 0.012.
Values may be sent and summed in bfloat16 or wider, within the bound.
A program may use at most 128 MiB of HBM per device.

v0:
```python
import jax
import jax.numpy as jnp
from jax import lax
from jax.sharding import PartitionSpec as P

MICRO = 2
CAP = 20


def together(arrays, axis):
    ravelled, at, gathered = (jnp.concatenate([a.reshape(-1) for a in arrays]), 0, [])
    subtotal = lax.psum(ravelled, axis)
    for a in arrays:
        gathered.append(subtotal[at : at + a.size].reshape(a.shape))
        at += a.size
    return tuple(gathered)


def slot_tables(route, prob):
    rows_count = route.shape[0]
    experts = prob.shape[-1]
    capacity = CAP
    flat = route.reshape(-1)
    onehot = (flat[:, None] == jnp.arange(experts, dtype=jnp.int32)[None, :]).astype(jnp.int32)
    before = jnp.cumsum(onehot, axis=0) - onehot
    place = jnp.sum(before * onehot, axis=1)
    slot = flat * capacity + place
    picked = jnp.take_along_axis(prob, route, axis=1)
    weights = picked / jnp.sum(picked, axis=1, keepdims=True)
    grid = (slot[:, None] == jnp.arange(experts * capacity, dtype=jnp.int32)[None, :]).astype(
        jnp.float32
    )
    grid = grid.reshape(rows_count, route.shape[1], experts * capacity)
    dispatch = jnp.sum(grid, axis=1).T.astype(jnp.bfloat16)
    combine = jnp.sum(grid * weights[:, :, None], axis=1)
    counts = jnp.sum(onehot, axis=0).astype(jnp.float32)
    return (dispatch, combine, counts)


def spread_slots(slots, experts, copies_per, capacity):
    width = slots.shape[-1]
    wide = jnp.broadcast_to(
        slots.reshape(experts, 1, capacity, width), (experts, copies_per, capacity, width)
    )
    return wide.reshape(experts * copies_per, capacity, width)


def local(tokens, routes, probs, w_gate, w_up, w_down):
    groups = lax.axis_size("dp")
    experts = probs.shape[-1]
    copies_per = groups // experts
    capacity = CAP
    gate_local = w_gate[0]
    up_local = w_up[0]
    down_local = w_down[0]
    rows_local = tokens.shape[1]
    total_rows = rows_local * groups
    top_count = routes.shape[-1]
    tables = [slot_tables(routes[index], probs[index]) for index in range(MICRO)]
    prob_local = [jnp.sum(probs[index], axis=0) for index in range(MICRO)]
    count_table, prob_table = together(
        (jnp.stack([tables[index][2] for index in range(MICRO)]), jnp.stack(prob_local)), "dp"
    )
    outputs = []
    loss_terms = []
    for micro_index in range(MICRO):
        dispatch, combine, counts = tables[micro_index]
        count_all = count_table[micro_index]
        prob_all = prob_table[micro_index]
        width_local = tokens.shape[2]
        slots = jnp.dot(dispatch, tokens[micro_index], preferred_element_type=jnp.float32).astype(
            jnp.bfloat16
        )
        arrived = lax.all_to_all(
            spread_slots(slots, experts, copies_per, capacity),
            "dp",
            split_axis=0,
            concat_axis=0,
            tiled=True,
        )
        piece = lax.all_gather(arrived, "tensor", axis=2, tiled=True)
        piece_rows = piece.reshape(-1, piece.shape[2])
        gate = jnp.dot(piece_rows, gate_local, preferred_element_type=jnp.float32)
        up = jnp.dot(piece_rows, up_local, preferred_element_type=jnp.float32)
        hidden = (jax.nn.silu(gate) * up).astype(jnp.bfloat16)
        part = jnp.dot(hidden, down_local, preferred_element_type=jnp.float32).astype(jnp.bfloat16)
        reduced = lax.psum_scatter(part, "tensor", scatter_dimension=1, tiled=True).astype(
            jnp.float32
        )
        returned = lax.all_to_all(
            reduced.reshape(groups, capacity, width_local).astype(jnp.bfloat16),
            "dp",
            split_axis=0,
            concat_axis=0,
            tiled=True,
        ).astype(jnp.float32)
        summed = jnp.sum(returned.reshape(experts, copies_per, capacity, width_local), axis=1)
        mixed = jnp.dot(
            combine,
            summed.reshape(experts * capacity, width_local),
            precision=lax.Precision.HIGHEST,
            preferred_element_type=jnp.float32,
        )
        outputs.append(mixed.astype(jnp.bfloat16))
        loss_terms.append(
            experts * (count_all / (total_rows * top_count)) * (prob_all / total_rows)
        )
    return (jnp.stack(outputs), jnp.stack(loss_terms))


def solution(mesh):
    in_specs = (
        P(None, "dp", "tensor"),
        P(None, "dp", None),
        P(None, "dp", None),
        P("dp", None, "tensor"),
        P("dp", None, "tensor"),
        P("dp", "tensor", None),
    )
    out_specs = (P(None, "dp", "tensor"), P())
    return jax.shard_map(local, mesh=mesh, in_specs=in_specs, out_specs=out_specs, check_vma=False)
```

profile of v0, /device:TPU:1, one launch (start us, length us, event | category | flops | bytes accessed | tf_op | source)
XLA Modules:
  0.0 393.9 jit_solution(13326397115779215763)
XLA Ops:
  7.2 0.7 fusion.46
  7.9 0.7 bitcast_or_fusion.1
  8.7 0.1 eq.58
  8.9 0.2 reduce_window_sum.17
  9.1 0.2 fusion.36
  9.3 0.1 reduce_sum.131
  9.6 0.2 eq.65
  9.9 0.2 reduce_window_sum.18
  10.0 0.2 fusion.37
  10.2 0.1 reduce_sum.137
  10.4 0.9 slice_reduce_fusion.1
  11.3 0.1 copy.34
  11.4 0.1 reshape.174
  11.5 1.0 gather_fusion
  12.6 0.1 reshape.177
  12.9 0.2 reshape.179
  13.0 1.0 gather_fusion.1
  14.1 0.1 reshape.182
  14.3 0.1 convert_reduce_fusion.2
  14.5 0.3 convolution_convert_fusion
  14.8 0.2 broadcast_in_dim.14
  15.0 32.2 %all_to_all.20 = bf16[32,20,1024]{2,1,0:T(8,128)(2,1)} all-to-all(bf16[32,20,1024]{2,1,0:T(8,128)(2,1)S(1)} %bitcast.97), channel_id=1, replica_groups=mesh['dp'=32,'tensor'=4] {'dp'}, dimensions={0} | all-to-all | bytes 2621440 | tf_op jit(solution)/shard_map/all_to_all | solution.py:74
  47.3 0.3 convolution_convert_fusion.1
  47.6 0.2 broadcast_in_dim.12
  47.8 26.4 %all_to_all.21 = bf16[32,20,1024]{2,1,0:T(8,128)(2,1)} all-to-all(bf16[32,20,1024]{2,1,0:T(8,128)(2,1)S(1)} %bitcast.98), channel_id=1, replica_groups=mesh['dp'=32,'tensor'=4] {'dp'}, dimensions={0} | all-to-all | bytes 2621440 | tf_op jit(solution)/shard_map/all_to_all | solution.py:74
  74.2 36.0 %all-gather.5.cloned.1.call-done = bf16[32,20,4096]{2,1,0:T(8,128)(2,1)} async-done(((bf16[32,20,1024]{2,1,0:T(8,128)(2,1)}), bf16[32,20,4096]{2,1,0:T(8,128)(2,1)}) %all-gather.5.cloned.1.call-update) | async-done | bytes 5242896 | tf_op jit(solution)/shard_map/all_gather | solution.py:81
  110.3 7.8 %reshape.140 = bf16[640,4096]{1,0:T(8,128)(2,1)} reshape(bf16[32,20,4096]{2,1,0:T(8,128)(2,1)} %all-gather.5.cloned.1.call-done) | data formatting | bytes 10485760 | tf_op jit(solution)/shard_map/reshape | solution.py:82
  118.0 11.7 %fusion.8 = f32[640,896]{1,0:T(8,128)S(1)} fusion(bf16[640,4096]{1,0:T(8,128)(2,1)} %reshape.140, bf16[1,4096,896]{2,1,0:T(8,128)(2,1)} %param.11), kind=kOutput, calls=%fused_computation.10 | convolution fusion | flops 4697620480 | bytes 14876672 | tf_op jit(solution)/shard_map/dot_general | solution.py:83
  129.7 18.9 %fusion.15 = bf16[640,4096]{1,0:T(8,128)(2,1)} fusion(bf16[1,896,4096]{2,1,0:T(8,128)(2,1)} %param.13, f32[640,896]{1,0:T(8,128)S(1)} %fusion.8, bf16[640,4096]{1,0:T(8,128)(2,1)} %reshape.140, bf16[1,4096,896]{2,1,0:T(8,128)(2,1)} %param.12), kind=kOutput, calls=%fused_computation.15 | convolution fusion | flops 9401303040 | bytes 27459584 | tf_op jit(solution)/shard_map/dot_general | solution.py:86
  148.6 0.2 reduce-scatter.3.cloned.1.call-start
  148.8 29.4 %all-gather.3.cloned.1.call-done = bf16[32,20,4096]{2,1,0:T(8,128)(2,1)} async-done(((bf16[32,20,1024]{2,1,0:T(8,128)(2,1)}), bf16[32,20,4096]{2,1,0:T(8,128)(2,1)}) %all-gather.3.cloned.1.call-update) | async-done | bytes 5242896 | tf_op jit(solution)/shard_map/all_gather | solution.py:81
  178.2 7.7 %reshape.135 = bf16[640,4096]{1,0:T(8,128)(2,1)} reshape(bf16[32,20,4096]{2,1,0:T(8,128)(2,1)} %all-gather.3.cloned.1.call-done) | data formatting | bytes 10485760 | tf_op jit(solution)/shard_map/reshape | solution.py:82
  185.9 11.6 %fusion.10 = f32[640,896]{1,0:T(8,128)S(1)} fusion(bf16[640,4096]{1,0:T(8,128)(2,1)} %reshape.135, bf16[1,4096,896]{2,1,0:T(8,128)(2,1)} %param.11), kind=kOutput, calls=%fused_computation.12 | convolution fusion | flops 4697620480 | bytes 14876672 | tf_op jit(solution)/shard_map/dot_general | solution.py:83
  197.5 18.9 %fusion.12 = bf16[640,4096]{1,0:T(8,128)(2,1)} fusion(bf16[1,896,4096]{2,1,0:T(8,128)(2,1)} %param.13, f32[640,896]{1,0:T(8,128)S(1)} %fusion.10, bf16[640,4096]{1,0:T(8,128)(2,1)} %reshape.135, bf16[1,4096,896]{2,1,0:T(8,128)(2,1)} %param.12), kind=kOutput, calls=%fused_computation.14 | convolution fusion | flops 9401303040 | bytes 27459584 | tf_op jit(solution)/shard_map/dot_general | solution.py:86
  216.4 20.4 %reduce-scatter.5.cloned.1.call-done = bf16[640,1024]{1,0:T(8,128)(2,1)} async-done(((bf16[640,4096]{1,0:T(8,128)(2,1)}), bf16[640,1024]{1,0:T(8,128)(2,1)}) %reduce-scatter.5.cloned.1.call-update) | async-done | bytes 1310736 | tf_op jit(solution)/shard_map/reduce_scatter | solution.py:87
  236.8 3.2 convert_element_type.98
  240.0 7.7 %all-to-all-start.3 = ((bf16[32,20,1024]{2,1,0:T(8,128)(2,1)}), bf16[32,20,1024]{2,1,0:T(8,128)(2,1)S(1)}, u32[]{:S(2)}, u32[]{:S(2)}) async-start(bf16[32,20,1024]{2,1,0:T(8,128)(2,1)} %convert_element_type.98), calls=%async_computation.5 | async-start | bytes 3145728 | tf_op jit(solution)/shard_map/all_to_all | solution.py:90
  247.7 46.5 %reduce-scatter.3.cloned.1.call-done = bf16[640,1024]{1,0:T(8,128)(2,1)} async-done(((bf16[640,4096]{1,0:T(8,128)(2,1)}), bf16[640,1024]{1,0:T(8,128)(2,1)}) %reduce-scatter.3.cloned.1.call-update) | async-done | bytes 1310736 | tf_op jit(solution)/shard_map/reduce_scatter | solution.py:87
  294.3 3.2 convert_element_type.90
  297.5 7.7 %all-to-all-start.1 = ((bf16[32,20,1024]{2,1,0:T(8,128)(2,1)}), bf16[32,20,1024]{2,1,0:T(8,128)(2,1)S(1)}, u32[]{:S(2)}, u32[]{:S(2)}) async-start(bf16[32,20,1024]{2,1,0:T(8,128)(2,1)} %convert_element_type.90), calls=%async_computation.2 | async-start | bytes 3145728 | tf_op jit(solution)/shard_map/all_to_all | solution.py:90
  305.5 76.7 %psum.7 = f32[32]{0:T(128)S(1)} all-reduce(f32[32]{0:T(128)S(1)} %pad_maximum_fusion.4), channel_id=1, replica_groups=mesh['dp'=32,'tensor'=4] {'dp'}, use_global_device_ids=true, to_apply=%region_18.20 | all-reduce | flops 32 | bytes 256 | tf_op jit(solution)/shard_map/psum | solution.py:12
  382.3 0.6 pad_maximum_fusion.3
  382.9 1.2 convert_reduce_fusion
  384.0 1.2 reshape.143
  385.2 0.3 convert_reduce_fusion.1
  385.6 0.5 fusion.29
  386.1 0.5 fusion.28
  386.6 0.7 pad_maximum_fusion
  (36 shorter events, 1.6 us)
Async XLA Ops:
  7.2 103.1 %all-gather.5.cloned.1.call-start = ((), (), s32[]{:S(2)}) async-start(), calls=%async_computation.8 | async-start | bytes 7864320 | tf_op jit(solution)/shard_map/all_gather | solution.py:81
  13.0 1.3 copy-start.1
  13.0 1.5 copy-start
  47.2 131.0 %all-gather.3.cloned.1.call-start = ((), (), s32[]{:S(2)}) async-start(), calls=%async_computation.6 | async-start | bytes 7864320 | tf_op jit(solution)/shard_map/all_gather | solution.py:81
  74.2 162.6 %reduce-scatter.5.cloned.1.call-start = ((), (), s32[]{:S(2)}) async-start(), calls=%async_computation.9 | async-start | bytes 6553600 | tf_op jit(solution)/shard_map/reduce_scatter | solution.py:87
  148.6 145.7 %reduce-scatter.3.cloned.1.call-start = ((), (), s32[]{:S(2)}) async-start(), calls=%async_computation.7 | async-start | bytes 6553600 | tf_op jit(solution)/shard_map/reduce_scatter | solution.py:87
  240.0 57.5 %all-to-all-start.3 = ((bf16[32,20,1024]{2,1,0:T(8,128)(2,1)}), bf16[32,20,1024]{2,1,0:T(8,128)(2,1)S(1)}, u32[]{:S(2)}, u32[]{:S(2)}) async-start(bf16[32,20,1024]{2,1,0:T(8,128)(2,1)} %convert_element_type.98), calls=%async_computation.5 | async-start | bytes 3145728 | tf_op jit(solution)/shard_map/all_to_all | solution.py:90
  297.5 87.7 %all-to-all-start.1 = ((bf16[32,20,1024]{2,1,0:T(8,128)(2,1)}), bf16[32,20,1024]{2,1,0:T(8,128)(2,1)S(1)}, u32[]{:S(2)}, u32[]{:S(2)}) async-start(bf16[32,20,1024]{2,1,0:T(8,128)(2,1)} %convert_element_type.90), calls=%async_computation.2 | async-start | bytes 3145728 | tf_op jit(solution)/shard_map/all_to_all | solution.py:90
Sparse Core Ops, SparseCore 0:
  47.3 62.8 all-gather.4
  111.9 66.2 all-gather.2
  180.6 56.1 reduce-scatter.4
  239.1 55.1 reduce-scatter.2
where the time goes:
time: 395 us; the launch traced here: 394 us
  blocking collectives  135 us (34%)
  waiting for transfers between devices  132 us (33%)
  matrix products  62.5 us (16%)
  local copies, waits for them, and re-layouts  28.3 us (7%)
  starting transfers between devices  15.8 us (4%)
  between operations  14 us (4%)
  other arithmetic  5.56 us (1%)
    psum x1, blocking collectives, together(): subtotal = lax.psum(ravelled, axis)  76.7 us
    reduce_scatter x2, waiting for transfers between devices, local(): lax.psum_scatter(part, 'tensor', scatter_dimension=1, tiled=True)  67 us
    all_gather x2, waiting for transfers between devices, local(): piece = lax.all_gather(arrived, 'tensor', axis=2, tiled=True)  65.4 us
    all_to_all x2, blocking collectives, local(): lax.all_to_all(spread_slots(slots, experts, copies_per, capacity), 'dp',...  58.5 us
    dot_general x2, matrix products, local(): jnp.dot(hidden, down_local, preferred_element_type=jnp.float32)  37.8 us
    dot_general x2, matrix products, local(): gate = jnp.dot(piece_rows, gate_local, preferred_element_type=jnp.float32)  23.2 us
    all_to_all x2, starting transfers between devices, local(): lax.all_to_all(reduced.reshape(groups, capacity, width_local).astype(jnp....  15.4 us
    reshape x2, local copies, waits for them, and re-layouts, local(): piece_rows = piece.reshape(-1, piece.shape[2])  15.4 us
  transfers between devices with their start and end apart: 6, of which 4 were waited for; matrix products, arithmetic and copies ran while one was open for 22% of the time, Pallas kernels for 0%

commit v1 on v0

--- a/solution.py
+++ b/solution.py
@@ -78,7 +78,7 @@
             concat_axis=0,
             tiled=True,
         )
-        piece = lax.all_gather(arrived, "tensor", axis=2, tiled=True)
+        piece = jnp.concatenate(lax.all_gather(arrived, "tensor"), axis=2)
         piece_rows = piece.reshape(-1, piece.shape[2])
         gate = jnp.dot(piece_rows, gate_local, preferred_element_type=jnp.float32)
         up = jnp.dot(piece_rows, up_local, preferred_element_type=jnp.float32)

time: 395 us -> 383 us (0.970)
  waiting for transfers between devices: 132 us -> 101 us
  local copies, waits for them, and re-layouts: 28.3 us -> 41.8 us
    all_gather x2, waiting for transfers between devices: 65.4 us -> 35.1 us  [local(): piece = jnp.concatenate(lax.all_gather(arrived, 'tensor'), axis=2)]
    unnamed x4 -> x18, local copies, waits for them, and re-layouts: 0.01 us -> 11.9 us
    dot_general x2, matrix products: 37.8 us -> 48.9 us  [local(): jnp.dot(hidden, down_local, preferred_element_type=jnp.float32)]
    dot_general x2, matrix products: 23.2 us -> 13.8 us  [local(): gate = jnp.dot(piece_rows, gate_local, preferred_element_type=jnp.float32)]
  transfers between devices with their start and end apart: 6 -> 6, of which waited for: 4 -> 4; matrix products, arithmetic and copies ran while one was open for 22% -> 25% of each run, Pallas kernels for 0% -> 0%
where the time goes in v1:
time: 383 us; the launch traced here: 378 us
  blocking collectives  135 us (35%)
  waiting for transfers between devices  101 us (26%)
  matrix products  64.2 us (17%)
  local copies, waits for them, and re-layouts  41.8 us (11%)
  starting transfers between devices  16 us (4%)
  between operations  14.3 us (4%)
  other arithmetic  5.54 us (1%)
    psum x1, blocking collectives, together(): subtotal = lax.psum(ravelled, axis)  76.7 us
    reduce_scatter x2, waiting for transfers between devices, local(): lax.psum_scatter(part, 'tensor', scatter_dimension=1, tiled=True)  66 us
    all_to_all x2, blocking collectives, local(): lax.all_to_all(spread_slots(slots, experts, copies_per, capacity), 'dp',...  58.3 us
    dot_general x2, matrix products, local(): jnp.dot(hidden, down_local, preferred_element_type=jnp.float32)  48.9 us
    all_gather x2, waiting for transfers between devices, local(): piece = jnp.concatenate(lax.all_gather(arrived, 'tensor'), axis=2)  35.1 us
    all_to_all x2, starting transfers between devices, local(): lax.all_to_all(reduced.reshape(groups, capacity, width_local).astype(jnp....  15.5 us
    dot_general x2, matrix products, local(): gate = jnp.dot(piece_rows, gate_local, preferred_element_type=jnp.float32)  13.8 us
    reshape x2, local copies, waits for them, and re-layouts, local(): piece = jnp.concatenate(lax.all_gather(arrived, 'tensor'), axis=2)  13.4 us
  transfers between devices with their start and end apart: 6, of which 4 were waited for; matrix products, arithmetic and copies ran while one was open for 25% of the time, Pallas kernels for 0%

profile of v1, /device:TPU:1, one launch (start us, length us, event | category | flops | bytes accessed | tf_op | source)
XLA Modules:
  0.0 378.0 jit_solution(11702474386999660970)
XLA Ops:
  7.2 0.7 fusion.46
  7.9 0.7 bitcast_or_fusion.1
  8.9 0.2 reduce_window_sum.17
  9.1 0.2 fusion.36
  9.6 0.2 eq.65
  9.9 0.2 reduce_window_sum.18
  10.0 0.2 fusion.37
  10.2 0.1 reduce_sum.137
  10.4 0.9 slice_reduce_fusion.1
  11.4 0.1 reshape.176
  11.5 1.0 gather_fusion
  12.9 0.2 reshape.181
  13.0 1.0 gather_fusion.1
  14.5 0.3 convolution_convert_fusion
  14.8 0.2 broadcast_in_dim.14
  15.0 32.0 %all_to_all.20 = bf16[32,20,1024]{2,1,0:T(8,128)(2,1)S(1)} all-to-all(bf16[32,20,1024]{2,1,0:T(8,128)(2,1)S(1)} %bitcast.111), channel_id=1, replica_groups=mesh['dp'=32,'tensor'=4] {'dp'}, dimensions={0} | all-to-all | bytes 2621440 | tf_op jit(solution)/shard_map/all_to_all | solution.py:74
  47.1 1.8 copy.74
  49.0 0.3 convolution_convert_fusion.1
  49.3 0.2 broadcast_in_dim.12
  49.5 26.3 %all_to_all.21 = bf16[32,20,1024]{2,1,0:T(8,128)(2,1)S(1)} all-to-all(bf16[32,20,1024]{2,1,0:T(8,128)(2,1)S(1)} %bitcast.112), channel_id=1, replica_groups=mesh['dp'=32,'tensor'=4] {'dp'}, dimensions={0} | all-to-all | bytes 2621440 | tf_op jit(solution)/shard_map/all_to_all | solution.py:74
  75.7 1.8 copy.68
  77.6 0.4 reduce-scatter.5.cloned.1.call-start
  78.0 25.2 %all-gather.7.cloned.1.call-done = bf16[128,20,1024]{2,0,1:T(8,128)(2,1)} async-done(((bf16[32,20,1024]{2,0,1:T(8,128)(2,1)}), bf16[128,20,1024]{2,0,1:T(8,128)(2,1)}) %all-gather.7.cloned.1.call-update) | async-done | bytes 5242896 | tf_op jit(solution)/shard_map/all_gather | solution.py:81
  103.2 6.7 %copy.75 = bf16[32,20,4,1024]{3,2,1,0:T(4,128)(2,1)S(1)} copy(bf16[32,20,4,1024]{3,0,2,1:T(8,128)(2,1)} %bitcast.114) | data formatting | bytes 10485760 | tf_op jit(solution)/shard_map/reshape | solution.py:81
  109.9 3.5 copy.77
  113.4 2.4 copy-done
  115.8 6.9 %fusion.8 = f32[640,896]{1,0:T(8,128)} fusion(bf16[640,4096]{1,0:T(8,128)(2,1)S(1)} %bitcast.115, bf16[1,4096,896]{2,1,0:T(8,128)(2,1)S(1)} %bitcast.122), kind=kOutput, calls=%fused_computation.10 | convolution fusion | flops 4697620480 | bytes 14876672 | tf_op jit(solution)/shard_map/dot_general | solution.py:83
  122.7 29.6 %fusion.15 = bf16[640,4096]{1,0:T(8,128)(2,1)} fusion(bf16[1,896,4096]{2,1,0:T(8,128)(2,1)} %param.13, f32[640,896]{1,0:T(8,128)} %fusion.8, bf16[640,4096]{1,0:T(8,128)(2,1)} %bitcast.116, bf16[1,4096,896]{2,1,0:T(8,128)(2,1)} %param.12), kind=kOutput, calls=%fused_computation.15 | convolution fusion | flops 9401303040 | bytes 27459584 | tf_op jit(solution)/shard_map/dot_general | solution.py:86
  152.4 9.9 %all-gather.5.cloned.1.call-done = bf16[128,20,1024]{2,0,1:T(8,128)(2,1)} async-done(((bf16[32,20,1024]{2,0,1:T(8,128)(2,1)}), bf16[128,20,1024]{2,0,1:T(8,128)(2,1)}) %all-gather.5.cloned.1.call-update) | async-done | bytes 5242896 | tf_op jit(solution)/shard_map/all_gather | solution.py:81
  162.3 6.7 %copy.69 = bf16[32,20,4,1024]{3,2,1,0:T(4,128)(2,1)S(1)} copy(bf16[32,20,4,1024]{3,0,2,1:T(8,128)(2,1)} %bitcast.113) | data formatting | bytes 10485760 | tf_op jit(solution)/shard_map/reshape | solution.py:81
  169.0 3.5 copy.76
  172.5 2.6 copy-done.1
  175.1 6.9 %fusion.10 = f32[640,896]{1,0:T(8,128)} fusion(bf16[640,4096]{1,0:T(8,128)(2,1)S(1)} %bitcast.117, bf16[1,4096,896]{2,1,0:T(8,128)(2,1)S(1)} %bitcast.124), kind=kOutput, calls=%fused_computation.12 | convolution fusion | flops 4697620480 | bytes 14876672 | tf_op jit(solution)/shard_map/dot_general | solution.py:83
  182.0 19.2 %fusion.12 = bf16[640,4096]{1,0:T(8,128)(2,1)} fusion(bf16[1,896,4096]{2,1,0:T(8,128)(2,1)} %param.13, f32[640,896]{1,0:T(8,128)} %fusion.10, bf16[640,4096]{1,0:T(8,128)(2,1)} %bitcast.118, bf16[1,4096,896]{2,1,0:T(8,128)(2,1)} %param.12), kind=kOutput, calls=%fused_computation.14 | convolution fusion | flops 9401303040 | bytes 27459584 | tf_op jit(solution)/shard_map/dot_general | solution.py:86
  201.3 19.5 %reduce-scatter.5.cloned.1.call-done = bf16[640,1024]{1,0:T(8,128)(2,1)} async-done(((bf16[640,4096]{1,0:T(8,128)(2,1)}), bf16[640,1024]{1,0:T(8,128)(2,1)}) %reduce-scatter.5.cloned.1.call-update) | async-done | bytes 1310736 | tf_op jit(solution)/shard_map/reduce_scatter | solution.py:87
  220.8 3.2 convert_element_type.98
  224.0 7.8 %all-to-all-start.3 = ((bf16[32,20,1024]{2,1,0:T(8,128)(2,1)}), bf16[32,20,1024]{2,1,0:T(8,128)(2,1)S(1)}, u32[]{:S(2)}, u32[]{:S(2)}) async-start(bf16[32,20,1024]{2,1,0:T(8,128)(2,1)} %convert_element_type.98), calls=%async_computation.5 | async-start | bytes 3145728 | tf_op jit(solution)/shard_map/all_to_all | solution.py:90
  231.7 46.5 %reduce-scatter.3.cloned.1.call-done = bf16[640,1024]{1,0:T(8,128)(2,1)} async-done(((bf16[640,4096]{1,0:T(8,128)(2,1)}), bf16[640,1024]{1,0:T(8,128)(2,1)}) %reduce-scatter.3.cloned.1.call-update) | async-done | bytes 1310736 | tf_op jit(solution)/shard_map/reduce_scatter | solution.py:87
  278.2 3.2 convert_element_type.90
  281.4 7.7 %all-to-all-start.1 = ((bf16[32,20,1024]{2,1,0:T(8,128)(2,1)}), bf16[32,20,1024]{2,1,0:T(8,128)(2,1)S(1)}, u32[]{:S(2)}, u32[]{:S(2)}) async-start(bf16[32,20,1024]{2,1,0:T(8,128)(2,1)} %convert_element_type.90), calls=%async_computation.2 | async-start | bytes 3145728 | tf_op jit(solution)/shard_map/all_to_all | solution.py:90
  289.5 76.7 %psum.7 = f32[32]{0:T(128)S(1)} all-reduce(f32[32]{0:T(128)S(1)} %pad_maximum_fusion.4), channel_id=1, replica_groups=mesh['dp'=32,'tensor'=4] {'dp'}, use_global_device_ids=true, to_apply=%region_18.20 | all-reduce | flops 32 | bytes 256 | tf_op jit(solution)/shard_map/psum | solution.py:12
  366.2 0.6 pad_maximum_fusion.3
  366.8 1.2 convert_reduce_fusion
  368.0 1.2 reshape.143
  369.2 0.3 convert_reduce_fusion.1
  369.5 0.5 fusion.29
  370.0 0.5 fusion.28
  370.5 0.7 pad_maximum_fusion
  (54 shorter events, 2.3 us)
Async XLA Ops:
  7.2 96.1 %all-gather.7.cloned.1.call-start = ((), (), s32[]{:S(2)}) async-start(), calls=%async_computation.9 | async-start | bytes 6553600 | tf_op jit(solution)/shard_map/all_gather | solution.py:81
  13.0 1.3 copy-start.3
  13.0 1.5 copy-start.2
  48.9 113.4 %all-gather.5.cloned.1.call-start = ((), (), s32[]{:S(2)}) async-start(), calls=%async_computation.8 | async-start | bytes 6553600 | tf_op jit(solution)/shard_map/all_gather | solution.py:81
  77.6 143.2 %reduce-scatter.5.cloned.1.call-start = ((), (), s32[]{:S(2)}) async-start(), calls=%async_computation.7 | async-start | bytes 6553600 | tf_op jit(solution)/shard_map/reduce_scatter | solution.py:87
  103.2 12.5 %slice-start = ((s8[7340032]{0:T(1024)(128)(4,1)}), s8[4194304]{0:T(1024)(128)(4,1)S(1)}, s32[]{:S(2)}) async-start(s8[7340032]{0:T(1024)(128)(4,1)} %bitcast.121), calls=%async_computation.10 | async-start | bytes 8388608
  109.9 5.9 %slice-start.1 = ((s8[7340032]{0:T(1024)(128)(4,1)}), s8[3145728]{0:T(1024)(128)(4,1)S(1)}, s32[]{:S(2)}) async-start(s8[7340032]{0:T(1024)(128)(4,1)} %bitcast.121), calls=%async_computation.11 | async-start | bytes 6291456
  113.4 2.4 copy-start
  152.4 125.9 %reduce-scatter.3.cloned.1.call-start = ((), (), s32[]{:S(2)}) async-start(), calls=%async_computation.6 | async-start | bytes 6553600 | tf_op jit(solution)/shard_map/reduce_scatter | solution.py:87
  162.3 12.8 %slice-start.2 = ((s8[7340032]{0:T(1024)(128)(4,1)}), s8[4194304]{0:T(1024)(128)(4,1)S(1)}, s32[]{:S(2)}) async-start(s8[7340032]{0:T(1024)(128)(4,1)} %bitcast.123), calls=%async_computation.12 | async-start | bytes 8388608
  169.0 6.1 %slice-start.3 = ((s8[7340032]{0:T(1024)(128)(4,1)}), s8[3145728]{0:T(1024)(128)(4,1)S(1)}, s32[]{:S(2)}) async-start(s8[7340032]{0:T(1024)(128)(4,1)} %bitcast.123), calls=%async_computation.13 | async-start | bytes 6291456
  172.5 2.6 copy-start.1
  224.0 57.5 %all-to-all-start.3 = ((bf16[32,20,1024]{2,1,0:T(8,128)(2,1)}), bf16[32,20,1024]{2,1,0:T(8,128)(2,1)S(1)}, u32[]{:S(2)}, u32[]{:S(2)}) async-start(bf16[32,20,1024]{2,1,0:T(8,128)(2,1)} %convert_element_type.98), calls=%async_computation.5 | async-start | bytes 3145728 | tf_op jit(solution)/shard_map/all_to_all | solution.py:90
  281.4 87.7 %all-to-all-start.1 = ((bf16[32,20,1024]{2,1,0:T(8,128)(2,1)}), bf16[32,20,1024]{2,1,0:T(8,128)(2,1)S(1)}, u32[]{:S(2)}, u32[]{:S(2)}) async-start(bf16[32,20,1024]{2,1,0:T(8,128)(2,1)} %convert_element_type.90), calls=%async_computation.2 | async-start | bytes 3145728 | tf_op jit(solution)/shard_map/all_to_all | solution.py:90
Sparse Core Ops, SparseCore 0:
  49.0 54.1 all-gather.6
  104.9 57.3 all-gather.4
  164.7 55.9 reduce-scatter.4
  223.0 55.1 reduce-scatter.2
